TPU v7x, 32 devices: a whole 2x2x4 slice. The times are simulated.
32 devices in a mesh: row: 4 (over y, x), col: 8 (over z, core).
Axes of the slice: x: 2, y: 2, z: 4, core: 2. Of those that a mesh axis runs over, the one named last changes fastest.
Arguments:
- psi: bfloat16 [8192, 8192], P(('row', 'col')), may hold values from -0.125 to 0.125
- hpsi: bfloat16 [8192, 128], P(('row', 'col')), may hold values from -0.796875 to 0.796875
- slab_counts: int32 [32], P(('row', 'col')), may hold values from 1 to 256, 6144 in all
- matrix: float32 [4, 2048, 8, 1024], P('row', None, 'col'), as said below
Outputs:
- reduced: float32 [4, 2048, 8, 1024], P('row', None, 'col')
Inputs may be any that keep to these rules, and one draw needn't show every extreme that they name: Slab k's live plane waves are its first slab_counts[k] slots; the rest are padding; the counts sum to 3 * 256 * 32 // 4. The stored matrix is symmetric.
All inputs are finite; a program needn't handle non-finite values.
Results may differ from a plain program's by a relative error of at most 0.0003.
Values sent between devices are 32-bit elements; how exact they have to be, the bound alone decides.
No kernel may reach another device: no remote copies, remote signals or barrier semaphores. Data moves between devices by JAX's collectives and lax.ppermute only.
A program may use at most 64 MiB of HBM per device.

v0:
```python
import jax
import jax.numpy as jnp
from jax import lax
from jax.sharding import PartitionSpec as P

TILE = 16
HIGH = lax.Precision.HIGHEST


def lower_solve(factor, rhs):
    return lax.linalg.triangular_solve(factor, rhs, left_side=True, lower=True)


def invert_shifted(shifted):
    normal = jnp.dot(shifted.T, shifted, precision=HIGH)
    factor = jnp.linalg.cholesky(normal)
    first = lower_solve(factor, shifted.T)
    return lax.linalg.triangular_solve(factor, first, left_side=True, lower=True, transpose_a=True)


def per_device(psi, hpsi, slab_counts, matrix):
    prow_id = lax.axis_index("row")
    pcol_id = lax.axis_index("col")
    n_row = lax.axis_size("row")
    n_col = lax.axis_size("col")
    slots = psi.shape[0]
    panel = hpsi.shape[1]
    local_rows = matrix.shape[1]
    local_cols = matrix.shape[3]
    tiles_r = local_rows // TILE
    tiles_c = local_cols // TILE
    valid = jnp.arange(slots, dtype=jnp.int32) < slab_counts[0]
    hcols = jnp.where(valid[:, None], hpsi, jnp.zeros_like(hpsi))
    local_r = jnp.arange(local_rows, dtype=jnp.int32)
    local_c = jnp.arange(local_cols, dtype=jnp.int32)
    row_global = (local_r // TILE * n_row + prow_id) * TILE + local_r % TILE
    col_global = (local_c // TILE * n_col + pcol_id) * TILE + local_c % TILE
    partial_value = lax.dot_general(
        psi, hcols, (((0,), (0,)), ((), ())), preferred_element_type=jnp.float32
    )
    whole = lax.psum(partial_value, ("row", "col"))
    prow = lax.dynamic_index_in_dim(
        whole.reshape(tiles_r, n_row, TILE, panel), prow_id, 1, keepdims=False
    ).reshape(local_rows, panel)
    scols = lax.dynamic_index_in_dim(
        whole.reshape(tiles_c, n_col, TILE, panel), pcol_id, 1, keepdims=False
    ).reshape(local_cols, panel)
    span = jnp.arange(panel, dtype=jnp.int32)
    lower_r = jnp.where((row_global >= panel)[:, None], prow, jnp.zeros_like(prow))
    lower_c = jnp.where((col_global >= panel)[:, None], scols, jnp.zeros_like(scols))
    top_select = (row_global[None, :] == panel + span[:, None]).astype(jnp.float32)
    gram_part = jnp.dot(lower_r.T, lower_r, precision=HIGH)
    top_part = jnp.dot(top_select, prow, precision=HIGH)
    gram, top_rows = lax.psum((gram_part, top_part), "row")
    factor = jnp.linalg.cholesky(gram)
    basis_r = lower_solve(factor, lower_r.T).T
    basis_c = lower_solve(factor, lower_c.T).T
    top = lower_solve(factor, top_rows.T).T
    inverse = invert_shifted(jnp.eye(panel, dtype=jnp.float32) - top)
    embed_r = (row_global[:, None] == panel + span[None, :]).astype(jnp.float32)
    embed_c = (col_global[:, None] == panel + span[None, :]).astype(jnp.float32)
    reflect_r = basis_r - embed_r
    reflect_c = basis_c - embed_c
    stored = matrix[0, :, 0, :]
    col_select = (col_global[None, :] == span[:, None]).astype(jnp.float32)
    row_select = (row_global[None, :] == span[:, None]).astype(jnp.float32)
    left = jnp.dot(prow, col_select, precision=HIGH)
    upper = lax.dot_general(row_select, scols, (((0,), (1,)), ((), ())), precision=HIGH)
    inside_r = (row_global < panel)[:, None]
    inside_c = (col_global < panel)[None, :]
    refreshed = jnp.where(
        inside_r & inside_c,
        0.5 * (left + upper),
        jnp.where(inside_c, left, jnp.where(inside_r, upper, stored)),
    )
    zpart = jnp.dot(refreshed, reflect_c, precision=HIGH)
    zrows = lax.psum(zpart, "col")
    upart = lax.dot_general(refreshed, reflect_r, (((0,), (0,)), ((), ())), precision=HIGH)
    ucols = lax.psum(upart, "row")
    wmat = lax.psum(jnp.dot(reflect_r.T, zrows, precision=HIGH), "row")
    core = jnp.dot(jnp.dot(inverse, wmat, precision=HIGH), inverse.T, precision=HIGH)
    first = jnp.dot(reflect_r, jnp.dot(inverse, ucols.T, precision=HIGH), precision=HIGH)
    second = jnp.dot(
        jnp.dot(zrows, inverse.T, precision=HIGH) - jnp.dot(reflect_r, core, precision=HIGH),
        reflect_c.T,
        precision=HIGH,
    )
    return (refreshed - first - second)[None, :, None, :]


def solution(mesh):
    in_specs = (
        P(("row", "col"), None),
        P(("row", "col"), None),
        P(("row", "col")),
        P("row", None, "col", None),
    )
    out_specs = P("row", None, "col", None)
    return jax.shard_map(
        per_device, mesh=mesh, in_specs=in_specs, out_specs=out_specs, check_vma=False
    )
```

profile of v0, /device:TPU:0, one launch (start us, length us, event | category | flops | bytes accessed | tf_op | source)
XLA Modules:
  0.0 421.6 jit_solution(14257435263756658271)
XLA Ops:
  7.2 5.1 %convolution_bitcast_fusion = f32[8192,128]{0,1:T(8,128)} fusion(bf16[256,8192]{1,0:T(8,128)(2,1)} %param.7, bf16[256,128]{1,0:T(8,128)(2,1)} %param.8, pred[256]{0:T(512)(128)(4,1)S(1)} %iota_compare_fusion.9), kind=kOutput, calls=%fused_computation | convolution fusion | flops 536903680 | bytes 8454400 | tf_op jit(solution)/shard_map/dot_general | solution.py:38
  12.6 145.3 %all-reduce.6.cloned.1.call-done = f32[8192,128]{0,1:T(8,128)} async-done(((f32[8192,128]{0,1:T(8,128)}), f32[8192,128]{0,1:T(8,128)}) %all-reduce.6.cloned.1.call-update) | async-done | bytes 4194320 | tf_op jit(solution)/shard_map/psum | solution.py:41
  157.9 5.6 %copy.11 = f32[8192,128]{1,0:T(8,128)} copy(f32[8192,128]{0,1:T(8,128)} %all-reduce.6.cloned.1.call-done) | data formatting | bytes 8388608 | tf_op jit(solution)/shard_map/psum | solution.py:41
  163.4 1.6 broadcast_select_fusion
  165.0 2.4 convolution_bitcast_fusion.1
  167.5 3.6 fusion.10
  171.1 1.3 broadcast_select_fusion.1
  172.4 11.0 %fusion.1 = f32[2048,1024]{1,0:T(8,128)} fusion(f32[2048,1024]{1,0:T(8,128)S(1)} %fusion.10, f32[1,2048,1,1024]{3,2,1,0:T(1,128)} %param.10, pred[1024]{0:T(1024)(128)(4,1)S(1)} %broadcast_compare_fusion.1, pred[2048]{0:T(1024)(128)(4,1)S(1)} %broadcast_compare_fusion, f32[1024,128]{1,0:T(8,128)S(1)} %bitcast.89, s32[2048]{0:T(1024)S(1)} %fusion.60), kind=kOutput, calls=%fused_computation.3 | convolution fusion | flops 3234332672 | bytes 25701376 | tf_op jit(solution)/shard_map/dot_general | solution.py:68
  183.3 1.6 fusion.4
  185.0 23.8 %all-reduce.8.cloned.1.call-done = f32[128,128]{0,1:T(8,128)} async-done(((f32[128,128]{0,1:T(8,128)}), f32[128,128]{0,1:T(8,128)}) %all-reduce.8.cloned.1.call-update) | async-done | bytes 65552 | tf_op jit(solution)/shard_map/psum | solution.py:54
  208.8 0.9 copy.16
  209.7 0.9 fusion.29
  210.5 11.7 %cholesky.44 = f32[128,128]{1,0:T(8,128)S(1)} custom-call(f32[128,128]{1,0:T(8,128)S(1)} %fusion.29), custom_call_target="Cholesky" | custom-call | tf_op jit(solution)/shard_map/jit(cholesky)/cholesky | solution.py:55
  222.3 0.7 compare_reduce_fusion.1
  223.0 0.7 fusion.12
  223.7 9.8 %custom-call.13 = f32[1,128,128]{1,2,0:T(8,128)S(1)} custom-call(f32[1,128,128]{2,1,0:T(8,128)S(1)} %fusion.12), custom_call_target="InvertDiagBlocksLowerTriangular" | custom-call | tf_op jit(solution)/shard_map/triangular_solve | solution.py:11
  234.1 10.1 %fusion.77 = f32[2048,128]{1,0:T(8,128)} fusion(f32[2048,1024]{1,0:T(8,128)} %fusion.1, f32[1024,128]{1,0:T(8,128)S(1)} %convolution_subtract_fusion.2), kind=kOutput, calls=%fused_computation.122 | convolution fusion | flops 3221225472 | bytes 9961472 | tf_op jit(solution)/shard_map/dot_general | solution.py:76
  244.2 1.0 convolution_subtract_fusion.1
  245.2 16.6 %fusion.74 = f32[1024,128]{1,0:T(8,128)} fusion(f32[2048,1024]{1,0:T(8,128)} %fusion.1, f32[2048,128]{1,0:T(8,128)S(1)} %convolution_subtract_fusion.1), kind=kOutput, calls=%fused_computation.119 | convolution fusion | flops 3221225472 | bytes 9961472 | tf_op jit(solution)/shard_map/dot_general | solution.py:78
  261.8 41.8 %all-reduce.10.cloned.1.call-done = f32[2048,128]{1,0:T(8,128)} async-done(((f32[2048,128]{1,0:T(8,128)}), f32[2048,128]{1,0:T(8,128)}) %all-reduce.10.cloned.1.call-update) | async-done | bytes 1048592 | tf_op jit(solution)/shard_map/psum | solution.py:77
  303.7 3.7 fusion.79
  307.3 46.2 %all-reduce.12.cloned.1.call-done = (f32[128,128]{1,0:T(8,128)}, f32[1024,128]{1,0:T(8,128)}, f32[128,128]{1,0:T(8,128)}) async-done(((f32[128,128]{1,0:T(8,128)}, f32[1024,128]{1,0:T(8,128)}, f32[128,128]{1,0:T(8,128)}), (f32[128,128]{1,0:T(8,128)}, f32[1024,128]{1,0:T(8,128)}, f32[128,128]{1,0:T(8,128)})) %all-reduce.12.cloned.1.call-update) | async-done | bytes 655376 | tf_op jit(solution)/shard_map/psum | solution.py:54
  353.6 1.1 fusion.25
  355.1 11.7 %cholesky.55 = f32[128,128]{1,0:T(8,128)S(1)} custom-call(f32[128,128]{1,0:T(8,128)S(1)} %fusion.23), custom_call_target="Cholesky" | custom-call | tf_op jit(solution)/shard_map/jit(cholesky)/cholesky | solution.py:16
  368.0 9.8 %custom-call.14 = f32[1,128,128]{1,2,0:T(8,128)S(1)} custom-call(f32[1,128,128]{2,1,0:T(8,128)S(1)} %fusion.13), custom_call_target="InvertDiagBlocksLowerTriangular" | custom-call | tf_op jit(solution)/shard_map/triangular_solve | solution.py:18
  378.3 1.0 fusion.80
  379.7 1.8 fusion.75
  381.4 7.2 %fusion.76 = f32[2048,1024]{1,0:T(8,128)S(1)} fusion(f32[2048,128]{1,0:T(8,128)S(1)} %convolution_subtract_fusion.1, f32[128,1024]{1,0:T(8,128)S(1)} %fusion.75), kind=kOutput, calls=%fused_computation.121 | convolution fusion | flops 3221225472 | bytes 9961472 | tf_op jit(solution)/shard_map/dot_general | solution.py:82
  388.7 1.0 fusion.78
  389.7 1.0 convolution_subtract_fusion
  390.7 8.0 %subtract_bitcast_fusion = f32[1,2048,1,1024]{3,1,2,0:T(8,128)S(1)} fusion(f32[2048,1024]{1,0:T(8,128)S(1)} %bitcast.83, f32[2048,1024]{1,0:T(8,128)S(1)} %fusion.76, f32[2048,128]{1,0:T(8,128)S(1)} %convolution_subtract_fusion, f32[1024,128]{1,0:T(8,128)S(1)} %convolution_subtract_fusion.2), kind=kOutput, calls=%fused_computation.4 | convolution fusion | flops 3225419776 | bytes 26738688 | tf_op jit(solution)/shard_map/dot_general | solution.py:83
  398.7 16.1 %copy.18 = f32[1,2048,1,1024]{3,2,1,0:T(1,128)} copy(f32[1,2048,1,1024]{3,1,2,0:T(8,128)S(1)} %subtract_bitcast_fusion) | data formatting | bytes 16777216 | tf_op jit(solution)/shard_map/broadcast_in_dim | solution.py:88
  (34 shorter events, 3.3 us)
Async XLA Ops:
  6.5 151.3 %all-reduce.6.cloned.1.call-start = ((), (), s32[]{:S(2)}) async-start(), calls=%async_computation | async-start | bytes 8388608 | tf_op jit(solution)/shard_map/psum | solution.py:41
  12.3 196.4 %all-reduce.8.cloned.1.call-start = ((), (), s32[]{:S(2)}) async-start(), calls=%async_computation.1 | async-start | bytes 131072 | tf_op jit(solution)/shard_map/psum | solution.py:54
  167.5 136.2 %all-reduce.10.cloned.1.call-start = ((), (), s32[]{:S(2)}) async-start(), calls=%async_computation.2 | async-start | bytes 2097152 | tf_op jit(solution)/shard_map/psum | solution.py:77
  244.2 109.4 %all-reduce.12.cloned.1.call-start = ((), (), s32[]{:S(2)}) async-start(), calls=%async_computation.3 | async-start | bytes 1310720 | tf_op jit(solution)/shard_map/psum | solution.py:54
  379.6 9.0 %copy-start = (f32[2048,128]{1,0:T(8,128)S(1)}, f32[2048,128]{1,0:T(8,128)}, u32[]{:S(2)}) copy-start(f32[2048,128]{1,0:T(8,128)} %all-reduce.10.cloned.1.call-done) | copy-start | bytes 3145732
  379.6 11.0 %slice-start = ((s8[8388608]{0:T(1024)(128)(4,1)}), s8[4194304]{0:T(1024)(128)(4,1)S(1)}, s32[]{:S(2)}) async-start(s8[8388608]{0:T(1024)(128)(4,1)} %bitcast.82), calls=%async_computation.4 | async-start | bytes 8388608
  381.4 9.3 %slice-start.1 = ((s8[8388608]{0:T(1024)(128)(4,1)}), s8[4194304]{0:T(1024)(128)(4,1)S(1)}, s32[]{:S(2)}) async-start(s8[8388608]{0:T(1024)(128)(4,1)} %bitcast.82), calls=%async_computation.5 | async-start | bytes 8388608
Sparse Core Ops, SparseCore 0:
  12.9 144.9 all-reduce.5
  167.6 41.1 all-reduce.7
  244.3 59.2 all-reduce.9
  307.5 46.0 all-reduce.11
where the time goes:
time: 428 us; the launch traced here: 422 us
  waiting for transfers between devices  257 us (60%)
  matrix products  77.7 us (18%)
  other arithmetic  49.6 us (12%)
  local copies, waits for them, and re-layouts  22.7 us (5%)
  between operations  14.3 us (3%)
    psum x1, waiting for transfers between devices, per_device(): whole = lax.psum(partial_value, ('row', 'col'))  145 us
    psum x2, waiting for transfers between devices, per_device(): gram, top_rows = lax.psum((gram_part, top_part), 'row')  70 us
    psum x1, waiting for transfers between devices, per_device(): zrows = lax.psum(zpart, 'col')  41.8 us
    dot_general x1, matrix products, per_device(): lax.dot_general(refreshed, reflect_r, (((0,), (0,)), ((), ())), precision...  16.6 us
    broadcast_in_dim x1, local copies, waits for them, and re-layouts, per_device(): return (refreshed - first - second)[None, :, None, :]  16.1 us
    another operation x3, other arithmetic, per_device(): factor = jnp.linalg.cholesky(gram)  12.5 us
    another operation x3, other arithmetic, invert_shifted(): factor = jnp.linalg.cholesky(normal)  12.4 us
    dot_general x1, matrix products, per_device(): lax.dot_general(row_select, scols, (((0,), (1,)), ((), ())), precision=HIGH)  11 us
  transfers between devices with their start and end apart: 4, of which 4 were waited for; matrix products, arithmetic and copies ran while one was open for 8% of the time, Pallas kernels for 0%

commit v1 on v0

--- a/solution.py
+++ b/solution.py
@@ -74,7 +74,11 @@
         jnp.where(inside_c, left, jnp.where(inside_r, upper, stored)),
     )
     zpart = jnp.dot(refreshed, reflect_c, precision=HIGH)
-    zrows = lax.psum(zpart, "col")
+    size = lax.axis_size("col")
+    zrows, hop = (zpart, 1)
+    while hop < size:
+        zrows = zrows + lax.ppermute(zrows, "col", [(i, i ^ hop) for i in range(size)])
+        hop = 2 * hop
     upart = lax.dot_general(refreshed, reflect_r, (((0,), (0,)), ((), ())), precision=HIGH)
     ucols = lax.psum(upart, "row")
     wmat = lax.psum(jnp.dot(reflect_r.T, zrows, precision=HIGH), "row")

time: 428 us -> 446 us (1.042)
  waiting for transfers between devices: 257 us -> 273 us
    ppermute x0 -> x3, waiting for transfers between devices: none -> 54.5 us  [per_device(): lax.ppermute(zrows, 'col', [(i, i ^ hop) for i in range(size)])]
    psum x1 -> x0, waiting for transfers between devices: 41.8 us -> none  [per_device(): zrows = lax.psum(zpart, 'col')]
  transfers between devices with their start and end apart: 4 -> 6, of which waited for: 4 -> 6; matrix products, arithmetic and copies ran while one was open for 8% -> 8% of each run, Pallas kernels for 0% -> 0%
where the time goes in v1:
time: 446 us; the launch traced here: 440 us
  waiting for transfers between devices  273 us (61%)
  matrix products  74.8 us (17%)
  other arithmetic  49.8 us (11%)
  local copies, waits for them, and re-layouts  23.7 us (5%)
  between operations  14.6 us (3%)
    psum x1, waiting for transfers between devices, per_device(): whole = lax.psum(partial_value, ('row', 'col'))  146 us
    psum x2, waiting for transfers between devices, per_device(): gram, top_rows = lax.psum((gram_part, top_part), 'row')  72.5 us
    ppermute x3, waiting for transfers between devices, per_device(): lax.ppermute(zrows, 'col', [(i, i ^ hop) for i in range(size)])  54.5 us
    broadcast_in_dim x1, local copies, waits for them, and re-layouts, per_device(): return (refreshed - first - second)[None, :, None, :]  16.1 us
    dot_general x1, matrix products, per_device(): lax.dot_general(refreshed, reflect_r, (((0,), (0,)), ((), ())), precision...  14.5 us
    another operation x3, other arithmetic, invert_shifted(): factor = jnp.linalg.cholesky(normal)  12.5 us
    another operation x3, other arithmetic, per_device(): factor = jnp.linalg.cholesky(gram)  12.4 us
    dot_general x1, matrix products, per_device(): lax.dot_general(row_select, scols, (((0,), (1,)), ((), ())), precision=HIGH)  11 us
  transfers between devices with their start and end apart: 6, of which 6 were waited for; matrix products, arithmetic and copies ran while one was open for 8% of the time, Pallas kernels for 0%

profile of v1, /device:TPU:0, one launch (start us, length us, event | category | flops | bytes accessed | tf_op | source)
XLA Modules:
  0.0 439.7 jit_solution(13282865287849169796)
XLA Ops:
  7.2 5.1 %convolution_bitcast_fusion = f32[8192,128]{0,1:T(8,128)} fusion(bf16[256,8192]{1,0:T(8,128)(2,1)} %param.7, bf16[256,128]{1,0:T(8,128)(2,1)} %param.8, pred[256]{0:T(512)(128)(4,1)S(1)} %iota_compare_fusion.9), kind=kOutput, calls=%fused_computation | convolution fusion | flops 536903680 | bytes 8454400 | tf_op jit(solution)/shard_map/dot_general | solution.py:38
  12.6 145.6 %all-reduce.5.cloned.1.call-done = f32[8192,128]{0,1:T(8,128)} async-done(((f32[8192,128]{0,1:T(8,128)}), f32[8192,128]{0,1:T(8,128)}) %all-reduce.5.cloned.1.call-update) | async-done | bytes 4194320 | tf_op jit(solution)/shard_map/psum | solution.py:41
  158.2 5.6 %copy.11 = f32[8192,128]{1,0:T(8,128)} copy(f32[8192,128]{0,1:T(8,128)} %all-reduce.5.cloned.1.call-done) | data formatting | bytes 8388608 | tf_op jit(solution)/shard_map/psum | solution.py:41
  163.7 1.6 broadcast_select_fusion
  165.3 2.4 convolution_bitcast_fusion.1
  167.8 3.6 fusion.10
  171.4 1.3 broadcast_select_fusion.1
  172.7 11.0 %fusion.1 = f32[2048,1024]{1,0:T(8,128)} fusion(f32[2048,1024]{1,0:T(8,128)S(1)} %fusion.10, f32[1,2048,1,1024]{3,2,1,0:T(1,128)} %param.10, pred[1024]{0:T(1024)(128)(4,1)S(1)} %broadcast_compare_fusion.1, pred[2048]{0:T(1024)(128)(4,1)S(1)} %broadcast_compare_fusion, f32[1024,128]{1,0:T(8,128)S(1)} %bitcast.89, s32[2048]{0:T(1024)S(1)} %fusion.63), kind=kOutput, calls=%fused_computation.3 | convolution fusion | flops 3234332672 | bytes 25701376 | tf_op jit(solution)/shard_map/dot_general | solution.py:68
  183.7 25.3 %all-reduce.7.cloned.1.call-done = f32[128,128]{0,1:T(8,128)} async-done(((f32[128,128]{0,1:T(8,128)}), f32[128,128]{0,1:T(8,128)}) %all-reduce.7.cloned.1.call-update) | async-done | bytes 65552 | tf_op jit(solution)/shard_map/psum | solution.py:54
  210.8 11.7 %cholesky.44 = f32[128,128]{1,0:T(8,128)S(1)} custom-call(f32[128,128]{1,0:T(8,128)S(1)} %fusion.32), custom_call_target="Cholesky" | custom-call | tf_op jit(solution)/shard_map/jit(cholesky)/cholesky | solution.py:55
  223.8 9.8 %custom-call.13 = f32[1,128,128]{1,2,0:T(8,128)S(1)} custom-call(f32[1,128,128]{2,1,0:T(8,128)S(1)} %fusion.15), custom_call_target="InvertDiagBlocksLowerTriangular" | custom-call | tf_op jit(solution)/shard_map/triangular_solve | solution.py:11
  234.2 10.5 %fusion.80 = f32[2048,128]{1,0:T(8,128)S(1)} fusion(f32[2048,1024]{1,0:T(8,128)} %fusion.1, f32[1024,128]{1,0:T(8,128)S(1)} %convolution_subtract_fusion.2), kind=kOutput, calls=%fused_computation.125 | convolution fusion | flops 3221225472 | bytes 9961472 | tf_op jit(solution)/shard_map/dot_general | solution.py:76
  244.8 2.6 collective-permute-done
  247.5 1.6 collective-permute-start.1
  249.1 23.7 %collective-permute-done.1 = f32[2048,128]{1,0:T(8,128)S(1)} collective-permute-done((f32[2048,128]{1,0:T(8,128)S(1)}, f32[2048,128]{1,0:T(8,128)S(1)}, u32[]{:S(2)}, u32[]{:S(2)}) %collective-permute-start.1) | collective-permute-done | bytes 1048608 | tf_op jit(solution)/shard_map/ppermute | solution.py:80
  272.9 2.5 collective-permute-start.2
  275.4 1.7 fusion.4
  277.0 1.0 convolution_subtract_fusion.1
  278.0 14.5 %fusion.77 = f32[1024,128]{1,0:T(8,128)} fusion(f32[2048,1024]{1,0:T(8,128)S(1)} %bitcast.81, f32[2048,128]{1,0:T(8,128)S(1)} %convolution_subtract_fusion.1), kind=kOutput, calls=%fused_computation.122 | convolution fusion | flops 3221225472 | bytes 9961472 | tf_op jit(solution)/shard_map/dot_general | solution.py:82
  292.5 28.1 %collective-permute-done.2 = f32[2048,128]{1,0:T(8,128)S(1)} collective-permute-done((f32[2048,128]{1,0:T(8,128)S(1)}, f32[2048,128]{1,0:T(8,128)S(1)}, u32[]{:S(2)}, u32[]{:S(2)}) %collective-permute-start.2) | collective-permute-done | bytes 1048608 | tf_op jit(solution)/shard_map/ppermute | solution.py:80
  321.6 2.5 fusion.11
  324.1 47.1 %all-reduce.9.cloned.1.call-done = (f32[128,128]{1,0:T(8,128)}, f32[1024,128]{1,0:T(8,128)}, f32[128,128]{1,0:T(8,128)}) async-done(((f32[128,128]{1,0:T(8,128)}, f32[1024,128]{1,0:T(8,128)}, f32[128,128]{1,0:T(8,128)}), (f32[128,128]{1,0:T(8,128)}, f32[1024,128]{1,0:T(8,128)}, f32[128,128]{1,0:T(8,128)})) %all-reduce.9.cloned.1.call-update) | async-done | bytes 655376 | tf_op jit(solution)/shard_map/psum | solution.py:54
  371.3 1.1 fusion.28
  372.8 11.7 %cholesky.55 = f32[128,128]{1,0:T(8,128)S(1)} custom-call(f32[128,128]{1,0:T(8,128)S(1)} %fusion.26), custom_call_target="Cholesky" | custom-call | tf_op jit(solution)/shard_map/jit(cholesky)/cholesky | solution.py:16
  385.9 9.8 %custom-call.14 = f32[1,128,128]{1,2,0:T(8,128)S(1)} custom-call(f32[1,128,128]{2,1,0:T(8,128)S(1)} %fusion.16), custom_call_target="InvertDiagBlocksLowerTriangular" | custom-call | tf_op jit(solution)/shard_map/triangular_solve | solution.py:18
  396.3 1.0 fusion.81
  397.6 1.9 fusion.78
  399.5 1.0 fusion.83
  400.5 7.0 %fusion.79 = f32[2048,1024]{1,0:T(8,128)S(1)} fusion(f32[2048,128]{1,0:T(8,128)S(1)} %convolution_subtract_fusion.1, f32[128,1024]{1,0:T(8,128)S(1)} %fusion.78), kind=kOutput, calls=%fused_computation.124 | convolution fusion | flops 3221225472 | bytes 9961472 | tf_op jit(solution)/shard_map/dot_general | solution.py:86
  407.5 1.0 convolution_subtract_fusion
  408.6 8.0 %subtract_bitcast_fusion = f32[1,2048,1,1024]{3,1,2,0:T(8,128)S(1)} fusion(f32[2048,1024]{1,0:T(8,128)S(1)} %bitcast.83, f32[2048,1024]{1,0:T(8,128)S(1)} %fusion.79, f32[2048,128]{1,0:T(8,128)S(1)} %convolution_subtract_fusion, f32[1024,128]{1,0:T(8,128)S(1)} %copy-done.1), kind=kOutput, calls=%fused_computation.4 | convolution fusion | flops 3225419776 | bytes 26738688 | tf_op jit(solution)/shard_map/dot_general | solution.py:87
  416.6 16.1 %copy.18 = f32[1,2048,1,1024]{3,2,1,0:T(1,128)} copy(f32[1,2048,1,1024]{3,1,2,0:T(8,128)S(1)} %subtract_bitcast_fusion) | data formatting | bytes 16777216 | tf_op jit(solution)/shard_map/broadcast_in_dim | solution.py:92
  (50 shorter events, 7.7 us)
Async XLA Ops:
  6.5 151.6 %all-reduce.5.cloned.1.call-start = ((), (), s32[]{:S(2)}) async-start(), calls=%async_computation | async-start | bytes 8388608 | tf_op jit(solution)/shard_map/psum | solution.py:41
  12.3 196.7 %all-reduce.7.cloned.1.call-start = ((), (), s32[]{:S(2)}) async-start(), calls=%async_computation.1 | async-start | bytes 131072 | tf_op jit(solution)/shard_map/psum | solution.py:54
  167.8 203.5 %all-reduce.9.cloned.1.call-start = ((), (), s32[]{:S(2)}) async-start(), calls=%async_computation.2 | async-start | bytes 1310720 | tf_op jit(solution)/shard_map/psum | solution.py:54
  233.6 44.4 %slice-start = ((s8[8388608]{0:T(1024)(128)(4,1)}), s8[4194304]{0:T(1024)(128)(4,1)S(1)}, s32[]{:S(2)}) async-start(s8[8388608]{0:T(1024)(128)(4,1)} %bitcast.80), calls=%async_computation.3 | async-start | bytes 8388608
  234.2 42.9 %copy-start = (f32[1024,128]{1,0:T(8,128)}, f32[1024,128]{1,0:T(8,128)S(1)}, u32[]{:S(2)}) copy-start(f32[1024,128]{1,0:T(8,128)S(1)} %convolution_subtract_fusion.2) | copy-start | bytes 1572868
  234.2 43.8 %slice-start.1 = ((s8[8388608]{0:T(1024)(128)(4,1)}), s8[4194304]{0:T(1024)(128)(4,1)S(1)}, s32[]{:S(2)}) async-start(s8[8388608]{0:T(1024)(128)(4,1)} %bitcast.80), calls=%async_computation.4 | async-start | bytes 8388608
  244.7 2.7 collective-permute-start
  247.5 25.3 %collective-permute-start.1 = (f32[2048,128]{1,0:T(8,128)S(1)}, f32[2048,128]{1,0:T(8,128)S(1)}, u32[]{:S(2)}, u32[]{:S(2)}) collective-permute-start(f32[2048,128]{1,0:T(8,128)S(1)} %add.252), channel_id=1, source_target_pairs={{0,2},{1,3},{2,0},{3,1},{4,6},{5,7},{6,4},{7,5},{8,10},{9,11},{10,... | collective-permute-start | bytes 3145736 | tf_op jit(solution)/shard_map/ppermute | solution.py:80
  272.9 47.8 %collective-permute-start.2 = (f32[2048,128]{1,0:T(8,128)S(1)}, f32[2048,128]{1,0:T(8,128)S(1)}, u32[]{:S(2)}, u32[]{:S(2)}) collective-permute-start(f32[2048,128]{1,0:T(8,128)S(1)} %add.253), channel_id=1, source_target_pairs={{0,4},{1,5},{2,6},{3,7},{4,0},{5,1},{6,2},{7,3},{8,12},{9,13},{10,... | collective-permute-start | bytes 3145736 | tf_op jit(solution)/shard_map/ppermute | solution.py:80
  320.7 1.0 copy-start.2
  399.4 9.1 %slice-start.2 = ((s8[8388608]{0:T(1024)(128)(4,1)}), s8[4194304]{0:T(1024)(128)(4,1)S(1)}, s32[]{:S(2)}) async-start(s8[8388608]{0:T(1024)(128)(4,1)} %bitcast.82), calls=%async_computation.5 | async-start | bytes 8388608
  400.4 7.1 %copy-start.3 = (f32[2048,128]{1,0:T(8,128)S(1)}, f32[2048,128]{1,0:T(8,128)}, u32[]{:S(2)}) copy-start(f32[2048,128]{1,0:T(8,128)} %copy-done.2) | copy-start | bytes 3145732
  400.4 8.1 %slice-start.3 = ((s8[8388608]{0:T(1024)(128)(4,1)}), s8[4194304]{0:T(1024)(128)(4,1)S(1)}, s32[]{:S(2)}) async-start(s8[8388608]{0:T(1024)(128)(4,1)} %bitcast.82), calls=%async_computation.6 | async-start | bytes 8388608
  400.5 8.1 %copy-start.1 = (f32[1024,128]{1,0:T(8,128)S(1)}, f32[1024,128]{1,0:T(8,128)}, u32[]{:S(2)}) copy-start(f32[1024,128]{1,0:T(8,128)} %copy-done) | copy-start | bytes 1572868
Sparse Core Ops, SparseCore 0:
  12.9 145.2 all-reduce.4
  167.9 41.0 all-reduce.6
  324.3 46.9 all-reduce.8
